TPU v7x, 256 devices: a whole 4x4x8 slice. The times are simulated.
256 devices in a mesh: row: 8 (over y, core), col: 32 (over x, z).
Axes of the slice: x: 4, y: 4, z: 8, core: 2. Of those that a mesh axis runs over, the one named last changes fastest.
Arguments:
- sources: bfloat16 [8, 32, 4, 256, 256], P('row', 'col'), may hold values from -6 to 6
- history: bfloat16 [8, 32, 8, 256, 256], P(None, 'col'), may hold values from -4 to 4
- inverse_diagonal: float32 [8, 32, 256], P('row', 'col'), may hold values from 0.3 to 0.6
- far_cores: bfloat16 [8, 32, 32, 8, 32, 8, 32], P('row', None, None, None, 'col'), may hold values from -0.046875 to 0.046875
- target_basis: bfloat16 [8, 32, 256, 32], P('row', 'col'), may hold values from -1 to 1
- source_basis: bfloat16 [8, 32, 256, 32], P(None, 'col'), may hold values from -0.375 to 0.375
- near_blocks: bfloat16 [8, 32, 3, 256, 8, 256], P('row', 'col'), may hold values from -0.078125 to 0.078125
- near_tile: int32 [8, 32, 3], P('row', 'col'), may hold values from 0 to 7
- near_count: int32 [8, 32], P('row', 'col'), may hold values from 1 to 3, as said below
Outputs:
- new_steps: bfloat16 [8, 32, 4, 256, 256], P('row', 'col')
- energies: float32 [4, 256], replicated
Inputs may be any that keep to these rules, and one draw needn't show every extreme that they name: Only slots below near_count are used; in every draw some tile has all 3 slots live.
All inputs are finite; a program needn't handle non-finite values.
Results may differ from a plain program's by a relative error of at most 0.011.
Values may be sent and summed in bfloat16 or wider, within the bound.
A program may use at most 192 MiB of HBM per device.

v0:
```python
import jax
import jax.numpy as jnp
from jax import lax
from jax.sharding import Mesh
from jax.sharding import PartitionSpec as P

COL = ("col_0", "col_1")
ROW_COL = ("row_0", "row_1", "col_0", "col_1")
ROW = ("row_0", "row_1")


def in_blocks(shard, dim, count):
    dims = shard.shape
    blocks = shard.reshape(*dims[:dim], count, dims[dim] // count, *dims[dim + 1 :])
    return jnp.moveaxis(blocks, dim, 0)


def summed_on_arrival(shard, axis, dim):
    count = lax.axis_size(axis)
    blocks = lax.all_to_all(in_blocks(shard, dim, count), axis, 0, 0, tiled=True)
    return jnp.sum(blocks.astype(jnp.float32), axis=0)


def one_axis_at_a_time(shard, axes):
    for axis in axes:
        shard = lax.psum(shard, axis)
    return shard


def laid_out(blocks, dim):
    dims = list(blocks.shape[1:])
    dims[dim] *= blocks.shape[0]
    return jnp.moveaxis(blocks, 0, dim).reshape(dims)


def copy_for_each(shard, axis):
    count = lax.axis_size(axis)
    return lax.all_to_all(
        jnp.broadcast_to(shard[None], (count, *shard.shape)), axis, 0, 0, tiled=True
    )


def gathered_copies(shard, axis, dim):
    return laid_out(copy_for_each(shard, axis), dim)


def local(
    sources,
    history,
    inverse_diagonal,
    far_cores,
    target_basis,
    source_basis,
    near_blocks,
    near_tile,
    near_count,
):
    row_count = history.shape[0]
    col_count = far_cores.shape[1]
    rank_size = far_cores.shape[2]
    lag_count = history.shape[2]
    tile_size = history.shape[3]
    field_count = history.shape[4]
    step_count = sources.shape[2]
    panel_total = row_count * col_count * tile_size
    column_past = history[:, 0]
    basis = source_basis[:, 0]
    projected = jnp.einsum(
        "pta,pktx->pkax", basis, column_past, preferred_element_type=jnp.float32
    ).astype(jnp.bfloat16)
    core_matrix = far_cores.reshape(col_count * rank_size, row_count * lag_count * rank_size)
    own_basis = target_basis[0, 0]
    scaling = inverse_diagonal[0, 0][:, None]
    blocks_here = near_blocks[0, 0]
    tiles_here = near_tile[0, 0]
    live_count = near_count[0, 0]
    outputs = []
    energy_rows = []
    for moment in range(step_count):
        partial_value = jnp.dot(
            core_matrix,
            projected.reshape(row_count * lag_count * rank_size, field_count),
            preferred_element_type=jnp.float32,
        )

        def add_block(slot, total):
            source = lax.dynamic_index_in_dim(
                column_past, tiles_here[slot], 0, keepdims=False
            ).reshape(lag_count * tile_size, field_count)
            block = lax.dynamic_index_in_dim(blocks_here, slot, 0, keepdims=False).reshape(
                tile_size, lag_count * tile_size
            )
            return total + jnp.dot(block, source, preferred_element_type=jnp.float32)

        near = lax.fori_loop(
            0, live_count, add_block, jnp.zeros((tile_size, field_count), jnp.float32)
        )
        own_core = summed_on_arrival(partial_value.astype(jnp.bfloat16), COL, 0)
        far = jnp.dot(own_basis, own_core.astype(jnp.bfloat16), preferred_element_type=jnp.float32)
        fresh = (scaling * (sources[0, 0, moment].astype(jnp.float32) - far - near)).astype(
            jnp.bfloat16
        )
        outputs.append(fresh)
        squares = jnp.sum(jnp.square(fresh.astype(jnp.float32)), axis=0) / panel_total
        energy_rows.append(one_axis_at_a_time(squares, ROW_COL))
        if moment + 1 < step_count:
            gathered = gathered_copies(fresh[None], ROW, 0)
            column_past = jnp.concatenate([gathered[:, None], column_past[:, :-1]], axis=1)
            fresh_proj = jnp.einsum(
                "pta,ptx->pax", basis, gathered, preferred_element_type=jnp.float32
            ).astype(jnp.bfloat16)
            projected = jnp.concatenate([fresh_proj[:, None], projected[:, :-1]], axis=1)
    energies = jnp.stack(energy_rows, axis=0)
    new_steps = jnp.stack(outputs, axis=0)[None, None]
    return (new_steps, energies)


def solution(mesh):
    torus = Mesh(mesh.devices.reshape(4, 2, 4, 8), ("row_0", "row_1", "col_0", "col_1"))
    placed = (
        P(ROW, COL, None, None, None),
        P(None, COL, None, None, None),
        P(ROW, COL, None),
        P(ROW, None, None, None, COL, None, None),
        P(ROW, COL, None, None),
        P(None, COL, None, None),
        P(ROW, COL, None, None, None, None),
        P(ROW, COL, None),
        P(ROW, COL),
    )
    return jax.shard_map(
        local,
        mesh=torus,
        in_specs=placed,
        out_specs=(P(ROW, COL, None, None, None), P()),
        check_vma=False,
    )
```

profile of v0, /device:TPU:8, one launch (start us, length us, event | category | flops | bytes accessed | tf_op | source)
XLA Modules:
  0.0 313.3 jit_solution(5170817323404104412)
XLA Ops:
  0.6 22.6 %reshape.99 = bf16[1024,2048]{1,0:T(8,128)(2,1)} reshape(bf16[1,32,32,8,1,8,32]{6,5,4,3,2,1,0:T(8,128)(2,1)} %param.20) | data formatting | bytes 8388608 | tf_op jit(solution)/shard_map/reshape | solution.py:71
  23.3 5.1 %convolution_convert_fusion = bf16[8,8,256,32]{2,3,1,0:T(8,128)(2,1)S(1)} fusion(bf16[8,1,256,32]{2,3,1,0:T(8,128)(2,1)S(1)} %copy-done, bf16[8,1,8,256,256]{4,3,2,1,0:T(8,128)(2,1)} %param.18), kind=kOutput, calls=%fused_computation.38 | convolution fusion | flops 268959744 | bytes 9568256 | tf_op jit(solution)/shard_map/pta,pktx->pkax/dot_general | solution.py:68
  30.7 11.4 %all-to-all-start = ((bf16[32,32,256]{2,1,0:T(8,128)(2,1)}), bf16[32,32,256]{2,1,0:T(8,128)(2,1)}, u32[]{:S(2)}, u32[]{:S(2)}) async-start(bf16[32,32,256]{2,1,0:T(8,128)(2,1)} %bitcast.25), calls=%async_computation | async-start | bytes 1048576 | tf_op jit(solution)/shard_map/all_to_all | solution.py:20
  44.8 16.5 %while.40 = (s32[]{:T(128)}, f32[256,256]{1,0:T(8,128)S(1)}, s32[]{:T(128)}, bf16[3,256,8,256]{3,1,2,0:T(8,128)(2,1)S(1)}, s32[3]{0:T(128)}, /*index=5*/bf16[8,8...) while((s32[]{:T(128)}, f32[256,256]{1,0:T(8,128)S(1)}, s32[]{:T(128)}, ...), condition=%wide.region_2.3_spmd, body=%wide.region_1.2_spmd.sunk | while | flops 268500992 | bytes 2621629 | solution.py:95
  66.5 4.9 %all-to-all-start.1 = ((bf16[8,1,256,256]{3,2,1,0:T(8,128)(2,1)}), bf16[8,1,256,256]{3,2,1,0:T(8,128)(2,1)}, u32[]{:S(2)}, u32[]{:S(2)}) async-start(bf16[8,1,256,256]{3,2,1,0:T(8,128)(2,1)} %broadcast_in_dim.27), calls=%async_computation.1 | async-start | bytes 2097152 | tf_op jit(solution)/shard_map/all_to_all | solution.py:38
  71.4 6.9 %slice.41 = bf16[8,7,256,256]{3,2,1,0:T(8,128)(2,1)} slice(bf16[8,8,256,256]{3,2,1,0:T(8,128)(2,1)} %get-tuple-element.485), slice={[0:8], [0:7], [0:256], [0:256]} | slice | bytes 14680064 | tf_op jit(solution)/shard_map/slice | solution.py:108
  81.1 4.9 %all-to-all-done.1 = bf16[8,1,256,256]{3,2,1,0:T(8,128)(2,1)} async-done(((bf16[8,1,256,256]{3,2,1,0:T(8,128)(2,1)}), bf16[8,1,256,256]{3,2,1,0:T(8,128)(2,1)}, u32[]{:S(2)}, u32[]{:S(2)}) %all-to-all-start.1) | async-done | bytes 1048608 | tf_op jit(solution)/shard_map/all_to_all | solution.py:38
  95.1 9.4 %all-to-all-start.2 = ((bf16[32,32,256]{2,1,0:T(8,128)(2,1)}), bf16[32,32,256]{2,1,0:T(8,128)(2,1)}, u32[]{:S(2)}, u32[]{:S(2)}) async-start(bf16[32,32,256]{2,1,0:T(8,128)(2,1)} %bitcast.234), calls=%async_computation.2 | async-start | bytes 1048576 | tf_op jit(solution)/shard_map/all_to_all | solution.py:20
  104.6 7.5 %pad_maximum_fusion = bf16[8,8,256,256]{3,2,1,0:T(8,128)(2,1)} fusion(bf16[8,1,256,256]{3,2,1,0:T(8,128)(2,1)} %all-to-all-done.1, bf16[8,7,256,256]{3,2,1,0:T(8,128)(2,1)} %slice.41), kind=kLoop, calls=%fused_computation.29 | loop fusion | flops 4194304 | bytes 16777216 | tf_op jit(solution)/shard_map/concatenate | solution.py:108
  114.2 17.3 %while.41 = (s32[]{:T(128)}, f32[256,256]{1,0:T(8,128)S(1)}, s32[]{:T(128)}, bf16[3,256,8,256]{3,1,2,0:T(8,128)(2,1)S(1)}, s32[3]{0:T(128)}, /*index=5*/bf16[8,8...) while((s32[]{:T(128)}, f32[256,256]{1,0:T(8,128)S(1)}, s32[]{:T(128)}, ...), condition=%wide.region_5.6_spmd, body=%wide.region_4.5_spmd.sunk | while | flops 268500992 | bytes 2621629 | solution.py:95
  136.7 4.4 %all-to-all-start.3 = ((bf16[8,1,256,256]{3,2,1,0:T(8,128)(2,1)}), bf16[8,1,256,256]{3,2,1,0:T(8,128)(2,1)}, u32[]{:S(2)}, u32[]{:S(2)}) async-start(bf16[8,1,256,256]{3,2,1,0:T(8,128)(2,1)} %broadcast_in_dim.29), calls=%async_computation.3 | async-start | bytes 2097152 | tf_op jit(solution)/shard_map/all_to_all | solution.py:38
  141.1 6.4 %fusion.25 = bf16[8,7,256,256]{3,2,1,0:T(8,128)(2,1)} fusion(bf16[8,7,256,256]{3,2,1,0:T(8,128)(2,1)} %slice.41, bf16[8,1,256,256]{3,2,1,0:T(8,128)(2,1)} %all-to-all-done.1), kind=kLoop, calls=%fused_computation.36 | loop fusion | flops 3670016 | bytes 15728640 | tf_op jit(solution)/shard_map/concatenate | solution.py:108
  148.1 6.5 %all-to-all-done.3 = bf16[8,1,256,256]{3,2,1,0:T(8,128)(2,1)} async-done(((bf16[8,1,256,256]{3,2,1,0:T(8,128)(2,1)}), bf16[8,1,256,256]{3,2,1,0:T(8,128)(2,1)}, u32[]{:S(2)}, u32[]{:S(2)}) %all-to-all-start.3) | async-done | bytes 1048608 | tf_op jit(solution)/shard_map/all_to_all | solution.py:38
  163.7 11.0 %all-to-all-start.4 = ((bf16[32,32,256]{2,1,0:T(8,128)(2,1)}), bf16[32,32,256]{2,1,0:T(8,128)(2,1)}, u32[]{:S(2)}, u32[]{:S(2)}) async-start(bf16[32,32,256]{2,1,0:T(8,128)(2,1)} %bitcast.235), calls=%async_computation.4 | async-start | bytes 1048576 | tf_op jit(solution)/shard_map/all_to_all | solution.py:20
  174.8 7.5 %pad_maximum_fusion.1 = bf16[8,8,256,256]{3,2,1,0:T(8,128)(2,1)} fusion(bf16[8,1,256,256]{3,2,1,0:T(8,128)(2,1)} %all-to-all-done.3, bf16[8,7,256,256]{3,2,1,0:T(8,128)(2,1)} %fusion.25), kind=kLoop, calls=%fused_computation.31 | loop fusion | flops 4194304 | bytes 16777216 | tf_op jit(solution)/shard_map/concatenate | solution.py:108
  184.4 17.3 %while.42 = (s32[]{:T(128)}, f32[256,256]{1,0:T(8,128)S(1)}, s32[]{:T(128)}, bf16[3,256,8,256]{3,1,2,0:T(8,128)(2,1)S(1)}, s32[3]{0:T(128)}, /*index=5*/bf16[8,8...) while((s32[]{:T(128)}, f32[256,256]{1,0:T(8,128)S(1)}, s32[]{:T(128)}, ...), condition=%wide.region_8.9_spmd, body=%wide.region_7.8_spmd.sunk | while | flops 268500992 | bytes 2621629 | solution.py:95
  211.1 6.5 %fusion.24 = bf16[8,7,256,256]{3,2,1,0:T(8,128)(2,1)} fusion(bf16[8,7,256,256]{3,2,1,0:T(8,128)(2,1)} %fusion.25, bf16[8,1,256,256]{3,2,1,0:T(8,128)(2,1)} %all-to-all-done.3), kind=kLoop, calls=%fused_computation.35 | loop fusion | flops 3670016 | bytes 15728640 | tf_op jit(solution)/shard_map/concatenate | solution.py:108
  218.2 6.6 %all-to-all-done.5 = bf16[8,1,256,256]{3,2,1,0:T(8,128)(2,1)} async-done(((bf16[8,1,256,256]{3,2,1,0:T(8,128)(2,1)}), bf16[8,1,256,256]{3,2,1,0:T(8,128)(2,1)}, u32[]{:S(2)}, u32[]{:S(2)}) %all-to-all-start.5) | async-done | bytes 1048608 | tf_op jit(solution)/shard_map/all_to_all | solution.py:38
  233.9 11.0 %all-to-all-start.6 = ((bf16[32,32,256]{2,1,0:T(8,128)(2,1)}), bf16[32,32,256]{2,1,0:T(8,128)(2,1)}, u32[]{:S(2)}, u32[]{:S(2)}) async-start(bf16[32,32,256]{2,1,0:T(8,128)(2,1)} %bitcast.233), calls=%async_computation.6 | async-start | bytes 1048576 | tf_op jit(solution)/shard_map/all_to_all | solution.py:20
  244.9 7.3 %pad_maximum_fusion.2 = bf16[8,8,256,256]{3,2,1,0:T(8,128)(2,1)} fusion(bf16[8,7,256,256]{3,2,1,0:T(8,128)(2,1)} %fusion.24, bf16[8,1,256,256]{3,2,1,0:T(8,128)(2,1)} %all-to-all-done.5), kind=kLoop, calls=%fused_computation.32 | loop fusion | flops 4194304 | bytes 16777216 | tf_op jit(solution)/shard_map/concatenate | solution.py:108
  252.3 17.3 %while.43 = (s32[]{:T(128)}, f32[256,256]{1,0:T(8,128)S(1)}, s32[]{:T(128)}, bf16[3,256,8,256]{3,1,2,0:T(8,128)(2,1)S(1)}, s32[3]{0:T(128)}, /*index=5*/bf16[8,8...) while((s32[]{:T(128)}, f32[256,256]{1,0:T(8,128)S(1)}, s32[]{:T(128)}, ...), condition=%wide.region_11.12_spmd, body=%wide.region_10.11_spmd.sunk | while | flops 268500992 | bytes 2621629 | solution.py:95
  271.8 7.0 %all-reduce.2 = (f32[256]{0:T(256)S(1)}, f32[256]{0:T(256)S(1)}, f32[256]{0:T(256)S(1)}, f32[256]{0:T(256)S(1)}) all-reduce(f32[256]{0:T(256)S(1)} %broadcast_multiply_fusion, f32[256]{0:T(256)} %broadcast_multiply_fusion.1, f32[256]{0:T(256)} %broadcast_multiply_fusion.2, ...), channel_id=1, replica_groups=mesh['row_0'=4,'row_1'=2,'col_0'=4,'col_1'=8] {'row_0'}, use_global_device_ids=true, to_apply=%region_28.29 | all-reduce | flops 1024 | bytes 8192 | tf_op jit(solution)/shard_map/psum | solution.py:26
  281.3 10.6 %all-reduce.1 = (f32[256]{0:T(256)S(1)}, f32[256]{0:T(256)S(1)}, f32[256]{0:T(256)S(1)}, f32[256]{0:T(256)S(1)}) all-reduce(f32[256]{0:T(256)S(1)} %get-tuple-element.198, f32[256]{0:T(256)S(1)} %get-tuple-element.199, f32[256]{0:T(256)S(1)} %get-tuple-element.200, ...), channel_id=1, replica_groups=mesh['row_0'=4,'row_1'=2,'col_0'=4,'col_1'=8] {'col_0'}, use_global_device_ids=true, to_apply=%region_30.31 | all-reduce | flops 1024 | bytes 8192 | tf_op jit(solution)/shard_map/psum | solution.py:26
  291.9 18.9 %all-reduce = (f32[1,256]{1,0:T(1,128)S(1)}, f32[1,256]{1,0:T(1,128)S(1)}, f32[1,256]{1,0:T(1,128)S(1)}, f32[1,256]{1,0:T(1,128)S(1)}) all-reduce(f32[1,256]{1,0:T(1,128)S(1)} %bitcast.247, f32[1,256]{1,0:T(1,128)S(1)} %bitcast.248, f32[1,256]{1,0:T(1,128)S(1)} %bitcast.249, ...), channel_id=1, replica_groups=mesh['row_0'=4,'row_1'=2,'col_0'=4,'col_1'=8] {'col_1'}, use_global_device_ids=true, to_apply=%region_31.32 | all-reduce | flops 1024 | bytes 8192 | tf_op jit(solution)/shard_map/psum | solution.py:26
  (89 shorter events, 102.7 us)
Async XLA Ops:
  0.6 22.6 %copy-start = (bf16[8,1,256,32]{2,3,1,0:T(8,128)(2,1)S(1)}, bf16[8,1,256,32]{2,3,1,0:T(8,128)(2,1)}, u32[]{:S(2)}) copy-start(bf16[8,1,256,32]{2,3,1,0:T(8,128)(2,1)} %param.22) | copy-start | bytes 393220
  23.3 5.1 %copy-start.2 = (bf16[1024,2048]{1,0:T(8,128)(2,1)S(1)}, bf16[1024,2048]{1,0:T(8,128)(2,1)}, u32[]{:S(2)}) copy-start(bf16[1024,2048]{1,0:T(8,128)(2,1)} %reshape.99) | copy-start | bytes 12582916
  28.3 2.4 copy-start.1
  30.7 30.6 %all-to-all-start = ((bf16[32,32,256]{2,1,0:T(8,128)(2,1)}), bf16[32,32,256]{2,1,0:T(8,128)(2,1)}, u32[]{:S(2)}, u32[]{:S(2)}) async-start(bf16[32,32,256]{2,1,0:T(8,128)(2,1)} %bitcast.25), calls=%async_computation | async-start | bytes 1048576 | tf_op jit(solution)/shard_map/all_to_all | solution.py:20
  44.8 18.3 %copy-start.6 = (bf16[1,1,256,32]{2,3,1,0:T(8,128)(2,1)S(1)}, bf16[1,1,256,32]{2,3,1,0:T(8,128)(2,1)}, u32[]{:S(2)}) copy-start(bf16[1,1,256,32]{2,3,1,0:T(8,128)(2,1)} %param.21) | copy-start | bytes 49156
  64.8 0.7 copy-start.3
  66.5 19.5 %all-to-all-start.1 = ((bf16[8,1,256,256]{3,2,1,0:T(8,128)(2,1)}), bf16[8,1,256,256]{3,2,1,0:T(8,128)(2,1)}, u32[]{:S(2)}, u32[]{:S(2)}) async-start(bf16[8,1,256,256]{3,2,1,0:T(8,128)(2,1)} %broadcast_in_dim.27), calls=%async_computation.1 | async-start | bytes 2097152 | tf_op jit(solution)/shard_map/all_to_all | solution.py:38
  71.4 9.1 %copy-start.7 = (f32[256]{0:T(256)S(1)}, f32[256]{0:T(256)}, u32[]{:S(2)}) copy-start(f32[256]{0:T(256)} %get-tuple-element.208) | copy-start | bytes 3076
  95.1 36.4 %all-to-all-start.2 = ((bf16[32,32,256]{2,1,0:T(8,128)(2,1)}), bf16[32,32,256]{2,1,0:T(8,128)(2,1)}, u32[]{:S(2)}, u32[]{:S(2)}) async-start(bf16[32,32,256]{2,1,0:T(8,128)(2,1)} %bitcast.234), calls=%async_computation.2 | async-start | bytes 1048576 | tf_op jit(solution)/shard_map/all_to_all | solution.py:20
  135.0 0.6 copy-start.4
  136.7 17.9 %all-to-all-start.3 = ((bf16[8,1,256,256]{3,2,1,0:T(8,128)(2,1)}), bf16[8,1,256,256]{3,2,1,0:T(8,128)(2,1)}, u32[]{:S(2)}, u32[]{:S(2)}) async-start(bf16[8,1,256,256]{3,2,1,0:T(8,128)(2,1)} %broadcast_in_dim.29), calls=%async_computation.3 | async-start | bytes 2097152 | tf_op jit(solution)/shard_map/all_to_all | solution.py:38
  141.1 6.5 %copy-start.8 = (f32[256]{0:T(256)S(1)}, f32[256]{0:T(256)}, u32[]{:S(2)}) copy-start(f32[256]{0:T(256)} %get-tuple-element.206) | copy-start | bytes 3076
  163.7 38.0 %all-to-all-start.4 = ((bf16[32,32,256]{2,1,0:T(8,128)(2,1)}), bf16[32,32,256]{2,1,0:T(8,128)(2,1)}, u32[]{:S(2)}, u32[]{:S(2)}) async-start(bf16[32,32,256]{2,1,0:T(8,128)(2,1)} %bitcast.235), calls=%async_computation.4 | async-start | bytes 1048576 | tf_op jit(solution)/shard_map/all_to_all | solution.py:20
  205.2 0.7 copy-start.5
  206.9 17.9 %all-to-all-start.5 = ((bf16[8,1,256,256]{3,2,1,0:T(8,128)(2,1)}), bf16[8,1,256,256]{3,2,1,0:T(8,128)(2,1)}, u32[]{:S(2)}, u32[]{:S(2)}) async-start(bf16[8,1,256,256]{3,2,1,0:T(8,128)(2,1)} %broadcast_in_dim.31), calls=%async_computation.5 | async-start | bytes 2097152 | tf_op jit(solution)/shard_map/all_to_all | solution.py:38
  211.1 6.5 %copy-start.9 = (f32[256]{0:T(256)S(1)}, f32[256]{0:T(256)}, u32[]{:S(2)}) copy-start(f32[256]{0:T(256)} %get-tuple-element.204) | copy-start | bytes 3076
  233.9 35.6 %all-to-all-start.6 = ((bf16[32,32,256]{2,1,0:T(8,128)(2,1)}), bf16[32,32,256]{2,1,0:T(8,128)(2,1)}, u32[]{:S(2)}, u32[]{:S(2)}) async-start(bf16[32,32,256]{2,1,0:T(8,128)(2,1)} %bitcast.233), calls=%async_computation.6 | async-start | bytes 1048576 | tf_op jit(solution)/shard_map/all_to_all | solution.py:20
where the time goes:
time: 317 us; the launch traced here: 313 us
  local copies, waits for them, and re-layouts  61.6 us (19%)
  starting transfers between devices  56.4 us (18%)
  other arithmetic  53.9 us (17%)
  matrix products  50.3 us (16%)
  blocking collectives  39 us (12%)
  loops' own time  33.2 us (10%)
  waiting for transfers between devices  18 us (6%)
    all_to_all x4, starting transfers between devices, summed_on_arrival(): lax.all_to_all(in_blocks(shard, dim, count), axis, 0, 0, tiled=True)  42.9 us
    psum x4, blocking collectives, one_axis_at_a_time(): shard = lax.psum(shard, axis)  39 us
    concatenate x5, other arithmetic, local(): jnp.concatenate([gathered[:, None], column_past[:, :-1]], axis=1)  35.3 us
    another operation x4, loops' own time, local(): lax.fori_loop(0, live_count, add_block, jnp.zeros((tile_size, field_count...  33.2 us
    reshape x1, local copies, waits for them, and re-layouts, local(): far_cores.reshape(col_count * rank_size, row_count * lag_count * rank_size)  22.6 us
    dot_general x12, matrix products, add_block(): return total + jnp.dot(block, source, preferred_element_type=jnp.float32)  20.1 us
    all_to_all x3, waiting for transfers between devices, copy_for_each(): lax.all_to_all(jnp.broadcast_to(shard[None], (count, *shard.shape)), axis...  17.9 us
    dynamic_slice x12, local copies, waits for them, and re-layouts, add_block(): tiles_here[slot]  14.9 us
  transfers between devices with their start and end apart: 7, of which 3 were waited for; matrix products, arithmetic and copies ran while one was open for 28% of the time, Pallas kernels for 0%

commit v1 on v0

v1 whole, which is shorter than its diff:
```python
import functools

import jax
import jax.numpy as jnp
from jax import lax
from jax.experimental import pallas as pl
from jax.experimental.pallas import tpu as pltpu
from jax.sharding import PartitionSpec as P

BF = jnp.bfloat16
F32 = jnp.float32
NX, NY, NZ, NC = 4, 4, 8, 2
ROWS, COLS = NY * NC, NX * NZ
TILE, RANK, LAGS, STEPS, SLOTS, FIELDS = 256, 32, 8, 4, 3, 256
XROWS = NZ * RANK
HALF = XROWS // 2
DEPTH = ROWS * RANK
PANELS = ROWS * COLS * TILE


def dot(a, b):
    return jnp.dot(a, b, preferred_element_type=F32)


def kernel(
    tile_ref, count_ref, inv_ref, tbt_ref, sbt_ref,
    src_hbm, hist_hbm, cores_hbm, near_hbm,
    out_hbm, en_ref,
    raw, cores, past, nraw, near, proj, new0, new1, new2, new3, early,
    src, scale, tbasis, nacc, sb2, sbp, sbm, r1, r2, sfull, sz, rz, er0, er1, er2,
    raw_sem, hist_sem, near_sem, src_sem, out_sem,
    ag_s, ag_r, ug_s, ug_r, x_s, x_r, z_s, z_r, e_s, e_r,
):
    row, col = lax.axis_index("row"), lax.axis_index("col")
    y, c = row // NC, lax.rem(row, NC)
    x, z = col // NZ, lax.rem(col, NZ)
    news = (new0, new1, new2, new3)

    def at_row(d):
        return (lax.rem(row + d, ROWS), col)

    def at_y(d):
        return (lax.rem(y + d, NY) * NC + c, col)

    def at_x(d):
        return (row, lax.rem(x + d, NX) * NZ + z)

    def at_z(d):
        return (row, x * NZ + lax.rem(z + d, NZ))

    partner = (y * NC + 1 - c, col)

    def send(a, b, s, r, dev):
        copy = pltpu.make_async_remote_copy(
            src_ref=a, dst_ref=b, send_sem=s, recv_sem=r, device_id=dev,
            device_id_type=pl.DeviceIdType.MESH,
        )
        copy.start()
        return copy

    barrier = pltpu.get_barrier_semaphore()
    peers = [at_row(d) for d in range(1, ROWS)]
    peers += [at_x(d) for d in range(1, NX)] + [at_z(d) for d in range(1, NZ)]
    for dev in peers:
        pl.semaphore_signal(barrier, inc=1, device_id=dev, device_id_type=pl.DeviceIdType.MESH)

    def raw_copy(j):
        return pltpu.make_async_copy(cores_hbm.at[0, j, :, :, 0], raw.at[j], raw_sem.at[j])

    def hist_copy(g):
        p, t = g // LAGS, lax.rem(g, LAGS)
        return pltpu.make_async_copy(
            hist_hbm.at[p, 0, LAGS - 1 - t],
            past.at[p, pl.ds(pl.multiple_of(t * TILE, TILE), TILE)],
            hist_sem.at[g],
        )

    per = ROWS * LAGS // COLS

    def start_loads(j, carry):
        raw_copy(j).start()
        for h in range(per):
            hist_copy(per * j + h).start()
        return carry

    lax.fori_loop(0, COLS, start_loads, 0)
    near_copies = [
        pltpu.make_async_copy(near_hbm.at[0, 0, s], nraw.at[s], near_sem.at[s]) for s in range(SLOTS)
    ]
    for copy in near_copies:
        copy.start()
    src_copy = pltpu.make_async_copy(src_hbm.at[0, 0], src, src_sem)
    src_copy.start()

    r_id = lax.broadcasted_iota(jnp.int32, (TILE, TILE), 0)
    c_id = lax.broadcasted_iota(jnp.int32, (TILE, TILE), 1)
    spread = jnp.where(r_id == c_id, jnp.broadcast_to(inv_ref[0], (TILE, TILE)), 0.0)
    scale[...] = jnp.broadcast_to(jnp.sum(spread, axis=1, keepdims=True), (TILE, FIELDS))
    tbasis[...] = jnp.transpose(tbt_ref[...].astype(F32)).astype(BF)

    def prepare(j, carry):
        raw_copy(j).wait()
        for h in range(per):
            hist_copy(per * j + h).wait()
        base = (j // NZ) * XROWS + lax.rem(j, NZ) * (RANK // 2)
        base = pl.multiple_of(base, RANK // 2)
        block = raw.at[j]
        group = 128 // RANK
        for h in range(ROWS // group):
            wide = jnp.concatenate(
                [block[:, group * h + q].astype(F32) for q in range(group)], axis=-1
            )
            turned = jnp.swapaxes(wide, 0, 1)
            for k in range(LAGS):
                piece = turned[k].astype(BF)
                lane = (LAGS - 1 - k) * DEPTH + h * 128
                cores[pl.ds(base, RANK // 2), lane : lane + 128] = piece[: RANK // 2]
                cores[pl.ds(base + HALF, RANK // 2), lane : lane + 128] = piece[RANK // 2 :]
        for h in range(per):
            g = per * j + h
            p, t = g // LAGS, lax.rem(g, LAGS)
            tile = past[p, pl.ds(pl.multiple_of(t * TILE, TILE), TILE), :]
            value = dot(sbt_ref[p], tile).astype(BF)
            proj[pl.ds(pl.multiple_of(t * DEPTH + p * RANK, RANK), RANK), :] = value
        return carry

    lax.fori_loop(0, COLS, prepare, 0)

    def prepare_near():
        for s in range(SLOTS):
            near_copies[s].wait()
            live = (s < count_ref[0, 0]).astype(F32)

            def turn(i, carry):
                r0 = pl.multiple_of(i * 32, 32)
                turned = jnp.swapaxes(nraw[s, pl.ds(r0, 32)].astype(F32), 0, 1) * live
                for k in range(LAGS):
                    lane = (LAGS - 1 - k) * TILE
                    near[s, pl.ds(r0, 32), lane : lane + TILE] = turned[k].astype(BF)
                return carry

            lax.fori_loop(0, TILE // 32, turn, 0)

    def near_old(n):
        depth = (LAGS - n) * TILE
        for s in range(SLOTS):
            tile = tile_ref[0, 0, s]
            total = dot(near[s, :, :depth], past[tile, n * TILE :, :])
            for r in range(n - 1):
                lane = (LAGS - n + r) * TILE
                total = total + dot(near[s, :, lane : lane + TILE], news[r][tile])
            nacc[...] = total if s == 0 else nacc[...] + total

    def near_last(n):
        lane = (LAGS - 1) * TILE
        total = nacc[...]
        for s in range(SLOTS):
            total = total + dot(near[s, :, lane : lane + TILE], news[n - 1][tile_ref[0, 0, s]])
        nacc[...] = total

    def early_rows(n, lo, hi):
        def one(i, carry):
            rows = pl.ds(pl.multiple_of(i * XROWS, XROWS), XROWS)
            depth = (LAGS - 1) * DEPTH
            early[n % 2, rows, :] = dot(
                cores[rows, :depth], proj[n * DEPTH : n * DEPTH + depth, :]
            )
            return carry

        lax.fori_loop(lo, hi, one, 0)

    pl.semaphore_wait(barrier, len(peers))

    sent = []
    ag = []
    ug = []
    outs = []
    for n in range(STEPS):
        if n:
            for copy in ag:
                copy.wait_recv()

        def block(d):
            rows = pl.ds(pl.multiple_of(lax.rem(x + d, NX) * XROWS, XROWS), XROWS)
            if n == 0:
                return rows, dot(cores[rows, :], proj[: LAGS * DEPTH, :])
            depth = (LAGS - 1) * DEPTH
            late = dot(cores[rows, depth:], proj[(n + LAGS - 1) * DEPTH : (n + LAGS) * DEPTH, :])
            return rows, early[n % 2, rows, :] + late

        def half(d, h):
            return pl.ds(pl.multiple_of(lax.rem(x + d, NX) * XROWS + h * HALF, HALF), HALF)

        lo, hi = slice(0, HALF), slice(HALF, XROWS)
        lo, hi = pl.ds(0, HALF), pl.ds(HALF, HALF)
        _, value = block(2)
        sb2[n] = value.astype(BF)
        c0 = send(sb2.at[n, lo], r1.at[n, 0], x_s.at[n, 0], x_r.at[n, 0], at_x(1))
        c1 = send(sb2.at[n, hi], r1.at[n, 1], x_s.at[n, 1], x_r.at[n, 1], at_x(3))
        rows, value = block(1)
        sbp[n, HALF:, :] = value[HALF:].astype(BF)
        early[n % 2, half(1, 0), :] = value[:HALF]
        c2 = send(sbp.at[n, hi], r2.at[n, 0, hi], x_s.at[n, 2], x_r.at[n, 2], at_x(1))
        rows, value = block(3)
        sbm[n, :HALF, :] = value[:HALF].astype(BF)
        early[n % 2, half(3, 1), :] = value[HALF:]
        c3 = send(sbm.at[n, lo], r2.at[n, 1, lo], x_s.at[n, 3], x_r.at[n, 3], at_x(3))
        rows, value = block(0)
        early[n % 2, rows, :] = value

        if n == 0:
            prepare_near()
        else:
            near_old(n)

        c0.wait_recv()
        sbp[n, :HALF, :] = (early[n % 2, half(1, 0), :] + r1[n, 0].astype(F32)).astype(BF)
        c4 = send(sbp.at[n, lo], r2.at[n, 0, lo], x_s.at[n, 4], x_r.at[n, 4], at_x(1))
        c1.wait_recv()
        sbm[n, HALF:, :] = (early[n % 2, half(3, 1), :] + r1[n, 1].astype(F32)).astype(BF)
        c5 = send(sbm.at[n, hi], r2.at[n, 1, hi], x_s.at[n, 5], x_r.at[n, 5], at_x(3))
        sent += [c0, c1, c2, c3, c4, c5]

        if n == 0:
            near_old(0)
        elif n + 1 < STEPS:
            early_rows(n + 1, 0, 2)

        for h, copies in ((0, (c3, c4)), (1, (c2, c5))):
            for copy in copies:
                copy.wait_recv()
            part = slice(h * HALF, (h + 1) * HALF)
            total = early[n % 2, half(0, h), :] + r2[n, 0, part, :].astype(F32)
            total = total + r2[n, 1, part, :].astype(F32)
            total = total.reshape(NZ, RANK // 2, FIELDS)
            lanes = slice(h * (RANK // 2), (h + 1) * (RANK // 2))
            sfull[:, lanes, :] = total
            sz[n, :, lanes, :] = total.astype(BF)
        zc = []
        for d in (4, 3, 5, 2, 6, 1, 7):
            zt = lax.rem(z + d, NZ)
            zc.append(
                send(sz.at[n, zt], rz.at[n, d], z_s.at[n, d - 1], z_r.at[n, d - 1], at_z(d))
            )
        sent += zc

        if n + 1 < STEPS:
            early_rows(n + 1, 0 if n == 0 else 2, NX)
        if n:
            for dy in range(1, NY):
                ug[dy - 1].wait_recv()
                got = lax.rem(y - dy + NY, NY) * NC + c
                ug.append(
                    send(
                        news[n - 1].at[got], news[n - 1].at[got],
                        ug_s.at[n - 1, 3 + dy], ug_r.at[n - 1, 3 + dy], partner,
                    )
                )
            for copy in ug[3:]:
                copy.wait_recv()
            sent += ug
            near_last(n)

        if n == 0:
            src_copy.wait()
        base = src[n].astype(F32) - nacc[...]
        nacc[...] = base
        for copy in zc:
            copy.wait_recv()
        core = sfull[z]
        for d in range(1, NZ):
            core = core + rz[n, d].astype(F32)
        far = dot(tbasis[...], core.astype(BF))
        fresh = (scale[...] * (nacc[...] - far)).astype(BF)
        dest = news[n].at[row] if n + 1 < STEPS else news[n]
        dest[...] = fresh
        if n + 1 < STEPS:
            mine = pl.ds(pl.multiple_of((LAGS + n) * DEPTH + row * RANK, RANK), RANK)
            proj[mine, :] = dot(sbt_ref[row], fresh).astype(BF)
            ag = [
                send(proj.at[mine], proj.at[mine], ag_s.at[n, d - 1], ag_r.at[n, d - 1], at_row(d))
                for d in (4, 3, 5, 2, 6, 1, 7)
            ]
            sent += ag
            ug = [
                send(dest, dest, ug_s.at[n, dy - 1], ug_r.at[n, dy - 1], at_y(dy))
                for dy in range(1, NY)
            ]
            ug.append(send(dest, dest, ug_s.at[n, 3], ug_r.at[n, 3], partner))
        wide = fresh.astype(F32)
        er0[row, n : n + 1, :] = jnp.sum(wide * wide, axis=0, keepdims=True) / PANELS
        out = pltpu.make_async_copy(dest, out_hbm.at[0, 0, n], out_sem.at[n])
        out.start()
        outs.append(out)

    def spread_sum(buf, mine, count, first, target):
        copies = [
            send(buf.at[mine], buf.at[mine], e_s.at[first + d - 1], e_r.at[first + d - 1], target(d))
            for d in range(1, count)
        ]
        for copy in copies:
            copy.wait_recv()
        total = buf[0]
        for i in range(1, count):
            total = total + buf[i]
        return total, copies

    total, copies = spread_sum(er0, row, ROWS, 0, at_row)
    sent += copies
    er1[x] = total
    total, copies = spread_sum(er1, x, NX, ROWS - 1, at_x)
    sent += copies
    er2[z] = total
    total, copies = spread_sum(er2, z, NZ, ROWS + NX - 2, at_z)
    sent += copies
    en_ref[...] = total
    for copy in sent:
        copy.wait_send()
    for copy in outs:
        copy.wait()


def local(
    sources, history, inverse_diagonal, far_cores, target_basis, source_basis,
    near_blocks, near_tile, near_count,
):
    smem = pl.BlockSpec(memory_space=pltpu.SMEM)
    vmem = pl.BlockSpec(memory_space=pltpu.VMEM)
    hbm = pl.BlockSpec(memory_space=pl.ANY)
    dma = pltpu.SemaphoreType.DMA
    tile = (TILE, FIELDS)
    new_steps, energies = pl.pallas_call(
        kernel,
        out_shape=(
            jax.ShapeDtypeStruct((1, 1, STEPS, *tile), BF),
            jax.ShapeDtypeStruct((STEPS, FIELDS), F32),
        ),
        in_specs=[smem, smem, vmem, vmem, vmem, hbm, hbm, hbm, hbm],
        out_specs=(hbm, vmem),
        scratch_shapes=[
            pltpu.VMEM((COLS, RANK, ROWS, LAGS, RANK), BF),
            pltpu.VMEM((COLS * RANK, LAGS * DEPTH), BF),
            pltpu.VMEM((ROWS, LAGS * TILE, FIELDS), BF),
            pltpu.VMEM((SLOTS, TILE, LAGS, TILE), BF),
            pltpu.VMEM((SLOTS, TILE, LAGS * TILE), BF),
            pltpu.VMEM(((LAGS + STEPS - 1) * DEPTH, FIELDS), BF),
            pltpu.VMEM((ROWS, *tile), BF),
            pltpu.VMEM((ROWS, *tile), BF),
            pltpu.VMEM((ROWS, *tile), BF),
            pltpu.VMEM(tile, BF),
            pltpu.VMEM((2, COLS * RANK, FIELDS), F32),
            pltpu.VMEM((STEPS, *tile), BF),
            pltpu.VMEM(tile, F32),
            pltpu.VMEM((TILE, RANK), BF),
            pltpu.VMEM(tile, F32),
            pltpu.VMEM((STEPS, XROWS, FIELDS), BF),
            pltpu.VMEM((STEPS, XROWS, FIELDS), BF),
            pltpu.VMEM((STEPS, XROWS, FIELDS), BF),
            pltpu.VMEM((STEPS, 2, HALF, FIELDS), BF),
            pltpu.VMEM((STEPS, 2, XROWS, FIELDS), BF),
            pltpu.VMEM((NZ, RANK, FIELDS), F32),
            pltpu.VMEM((STEPS, NZ, RANK, FIELDS), BF),
            pltpu.VMEM((STEPS, NZ, RANK, FIELDS), BF),
            pltpu.VMEM((ROWS, STEPS, FIELDS), F32),
            pltpu.VMEM((NX, STEPS, FIELDS), F32),
            pltpu.VMEM((NZ, STEPS, FIELDS), F32),
            dma((COLS,)), dma((ROWS * LAGS,)), dma((SLOTS,)), dma, dma((STEPS,)),
            dma((STEPS, 7)), dma((STEPS, 7)), dma((STEPS, 7)), dma((STEPS, 7)),
            dma((STEPS, 6)), dma((STEPS, 6)), dma((STEPS, 7)), dma((STEPS, 7)),
            dma((17,)), dma((17,)),
        ],
        compiler_params=pltpu.CompilerParams(
            collective_id=0, has_side_effects=True, vmem_limit_bytes=60 << 20
        ),
    )(
        near_tile, near_count, inverse_diagonal[0],
        jnp.swapaxes(target_basis, 2, 3)[0, 0], jnp.swapaxes(source_basis, 2, 3)[:, 0],
        sources, history, far_cores, near_blocks,
    )
    return new_steps, energies


def solution(mesh):
    placed = (
        P("row", "col", None, None, None),
        P(None, "col", None, None, None),
        P("row", "col", None),
        P("row", None, None, None, "col", None, None),
        P("row", "col", None, None),
        P(None, "col", None, None),
        P("row", "col", None, None, None, None),
        P("row", "col", None),
        P("row", "col"),
    )
    return jax.shard_map(
        local,
        mesh=mesh,
        in_specs=placed,
        out_specs=(P("row", "col", None, None, None), P()),
        check_vma=False,
    )
```

time: 317 us -> 103 us (0.32)
  the two profiles are of different devices: /device:TPU:8 before, /device:TPU:1 now
where the time goes in v1:
time: 103 us
  Pallas kernels  98.3 us (95%)
  local copies, waits for them, and re-layouts  3.13 us (3%)
  between operations  1.29 us (1%)
    pallas_call x1, Pallas kernels, local(): pl.pallas_call(kernel, out_shape=(jax.ShapeDtypeStruct((1, 1, STEPS, *til...  98.3 us
    unnamed x2, local copies, waits for them, and re-layouts  3.13 us

profile of v1, /device:TPU:1, one launch (start us, length us, event | category | flops | bytes accessed | tf_op | source)
XLA Modules:
  0.0 102.7 jit_solution(11019419807295485515)
XLA Ops:
  1.3 98.3 %shard_map.104 = (bf16[1,1,4,256,256]{4,3,2,1,0:T(8,128)(2,1)}, f32[4,256]{1,0:T(4,128)}) custom-call(s32[1,1,3]{2,1,0:T(1,128)} %tile_ref.1, s32[1,1]{1,0:T(1,128)S(6)} %copy.14.count_ref, f32[1,256]{1,0:T(1,128)} %bitcast.11, bf16[32,256]{1,0:T(8,128)(2,1)} %bitcast.10, bf16[8,32,256]{2,1,0:T(8,128)(2,1)} %bitcast.9, bf16[1,1,4,256,256]{4,3,2,1,0:T(8,128)(2,1)} %src_hbm.1, ...), custom_call_target="tpu_custom_call" | custom-call | tf_op jit(solution)/shard_map/pallas_call | solution.py:332
  99.6 1.9 %copy.15 = bf16[1,1,4,256,256]{4,3,2,1,0:T(8,128)(2,1)} copy(bf16[1,1,4,256,256]{4,3,2,1,0:T(8,128)(2,1)} %get-tuple-element.4) | data formatting | bytes 1048576
  101.5 1.3 %copy.16 = f32[4,256]{1,0:T(4,128)} copy(f32[4,256]{1,0:T(4,128)} %get-tuple-element.5) | data formatting | bytes 8192
